TPU v7x, 32 devices: a whole 2x2x4 slice. The times are simulated.
32 devices in a mesh: fsdp: 4 (over y, x), width: 8 (over z, core).
Axes of the slice: x: 2, y: 2, z: 4, core: 2. Of those that a mesh axis runs over, the one named last changes fastest.
Arguments:
- train_gate: float32 [4096, 11008], P('fsdp', 'width'), may hold values from -0.125 to 0.125
- drift_gate: float32 [4096, 11008], P('fsdp', 'width'), may hold values from -0.09375 to 0.09375
- spread_gate: float32 [4096, 11008], P('fsdp', 'width'), may hold values from -0.09375 to 0.09375
- train_up: float32 [4096, 11008], P('fsdp', 'width'), may hold values from -0.125 to 0.125
- drift_up: float32 [4096, 11008], P('fsdp', 'width'), may hold values from -0.09375 to 0.09375
- spread_up: float32 [4096, 11008], P('fsdp', 'width'), may hold values from -0.09375 to 0.09375
- norm_train: float32 [4096], P(('fsdp', 'width')), may hold values from 0.25 to 1.75
- norm_step: float32 [4096], P(('fsdp', 'width')), may hold values from -0.3 to 0.3
Outputs:
- serving_gate: bfloat16 [4096, 11008], P(None, 'width')
- serving_up: bfloat16 [4096, 11008], P(None, 'width')
- scale_gate: float32 [11008], P('width')
- scale_up: float32 [11008], P('width')
- serve_norm: bfloat16 [4096], replicated
- whole_gate: float32 [4096, 11008], P('fsdp', 'width')
- whole_up: float32 [4096, 11008], P('fsdp', 'width')
All inputs are finite; a program needn't handle non-finite values.
Results may differ from a plain program's by a relative error of at most 0.0004.
Values may be sent and summed in bfloat16 or wider, within the bound.
A program may use at most 128 MiB of HBM per device.

v0:
```python
import functools

import jax
import jax.numpy as jnp
from jax import lax
from jax.experimental import pallas as pl
from jax.experimental.pallas import tpu as pltpu
from jax.sharding import PartitionSpec as P

learn_rate = 0.3
hold_rate = 0.9
LANES = 128
SUB = 16
MESH = pl.DeviceIdType.MESH


def ring_order(n):
    side = int(round(n**0.5))
    if side * side != n or side % 2:
        return list(range(n))
    walk = [y * side for y in range(side)]
    for y in reversed(range(side)):
        columns = range(1, side) if (side - 1 - y) % 2 == 0 else reversed(range(1, side))
        walk += [y * side + x for x in columns]
    return walk


def pick(table, index):
    value = jnp.int32(table[0])
    for k in range(1, len(table)):
        value = jnp.where(index == k, jnp.int32(table[k]), value)
    return value


def groups_of(columns):
    first = min(LANES, columns // 4 // LANES * LANES)
    second = min(3 * LANES, columns // 3 // LANES * LANES)
    cuts = [0] + [c for c in (first, first + second) if c] + [columns]
    gate = [(0, a, b - a) for a, b in zip(cuts, cuts[1:]) if b > a]
    return gate + [(1, 0, columns)]


def middle(columns):
    return columns // (2 * SUB) * SUB


def gather_kernel(n, w, order, names, *refs):
    (tg, dg, sg, tu, du, su, nt, ns) = refs[:8]
    (out_g, out_u, whole_g, whole_u, right_piece, left_piece, scale_out, norm_out) = refs[8:16]
    (tv, dv, sv, nv, passed, sums, q, scale_buf, norm_in, norm_buf) = refs[16:26]
    (in_sem, put_sem, piece_sem, small_sem, sum_send, sum_recv) = refs[26:32]
    (ring_send, ring_recv, nf_send, nf_recv, nw_send, nw_recv) = refs[32:]
    f_axis, w_axis = names
    columns, rows = tg.shape
    groups = groups_of(columns)
    last = len(groups) - 1
    args = ((tg, dg, sg), (tu, du, su))
    outs, wholes = (out_g, out_u), (whole_g, whole_u)
    me = lax.axis_index(f_axis)
    mw = lax.axis_index(w_axis)
    half_ring = n // 2
    at = {d: i for i, d in enumerate(order)}
    right = pick([order[(at[d] + 1) % n] for d in range(n)], me)
    left = pick([order[(at[d] - 1) % n] for d in range(n)], me)
    cut = middle(columns)

    loads = {}

    def load(g):
        m, c0, cn = groups[g]
        loads[g] = [
            pltpu.make_async_copy(
                args[m][k].at[pl.ds(c0, cn)], buf.at[m, pl.ds(c0, cn)], in_sem.at[k]
            )
            for k, buf in enumerate((tv, dv, sv))
        ]
        for copy in loads[g]:
            copy.start()

    barrier = pltpu.get_barrier_semaphore()
    for k in range(1, n):
        pl.semaphore_signal(
            barrier, inc=1, device_id={f_axis: lax.rem(me + k, n)}, device_id_type=MESH
        )
    load(0)
    above, below = mw < w - 1, mw > 0

    @pl.when(above)
    def _():
        pl.semaphore_signal(barrier, inc=1, device_id={w_axis: mw + 1}, device_id_type=MESH)

    @pl.when(below)
    def _():
        pl.semaphore_signal(barrier, inc=1, device_id={w_axis: mw - 1}, device_id_type=MESH)

    norm_loads = [
        pltpu.make_async_copy(x, norm_in.at[k], small_sem.at[k]) for k, x in enumerate((nt, ns))
    ]
    for copy in norm_loads:
        copy.start()
    q[...] = jnp.zeros_like(q)

    def blocks(c0, cn, body):
        full = cn // LANES

        @pl.loop(0, full)
        def _(b):
            body(pl.multiple_of(c0 + b * LANES, LANES), LANES)

        if cn % LANES:
            body(c0 + full * LANES, cn % LANES)

    def step_block(m, c, cn):
        for r in range(0, cn, SUB):
            at_rows = pl.ds(c + r, SUB)
            part = None
            for l in range(0, rows, LANES):
                lanes = pl.ds(l, LANES)
                hold = hold_rate * dv[m, at_rows, lanes] + sv[m, at_rows, lanes]
                new = tv[m, at_rows, lanes] - learn_rate * hold
                tv[m, at_rows, lanes] = new
                part = new * new if part is None else part + new * new
            q[pl.ds(r, SUB), :] = part
        sums[m, me, :, pl.ds(c, LANES)] = jnp.sum(q[...].T, axis=0, keepdims=True)

    def narrow_block(m, c, cn):
        lanes = pl.ds(c, LANES)
        total = sums[m, 0, :, lanes]
        for k in range(1, n):
            total = total + sums[m, k, :, lanes]
        scale = jnp.sqrt(total)
        scale_buf[m, :, lanes] = scale
        q[...] = jnp.broadcast_to(scale, (LANES, LANES)).T
        for r in range(0, cn, SUB):
            at_rows = pl.ds(c + r, SUB)
            by = q[pl.ds(r, SUB), :]
            for l in range(0, rows, LANES):
                lanes = pl.ds(l, LANES)
                nv[m, at_rows, lanes] = (tv[m, at_rows, lanes] / by).astype(jnp.bfloat16)

    puts = []
    sends = []

    def exchange(g):
        m, c0, cn = groups[g]
        lanes = pl.ds(c0, -(-cn // LANES) * LANES)
        for k in range(1, n):
            copy = pltpu.make_async_remote_copy(
                src_ref=sums.at[m, me, :, lanes],
                dst_ref=sums.at[m, me, :, lanes],
                send_sem=sum_send.at[g, k - 1],
                recv_sem=sum_recv.at[g, k - 1],
                device_id={f_axis: lax.rem(me + k, n)},
                device_id_type=MESH,
            )
            copy.start()
            sends.append(copy)

    def exchanged(g):
        m, c0, cn = groups[g]
        lanes = pl.ds(c0, -(-cn // LANES) * LANES)
        for k in range(1, n):
            come = lax.rem(me - k + n, n)
            pltpu.make_async_remote_copy(
                src_ref=sums.at[m, come, :, lanes],
                dst_ref=sums.at[m, come, :, lanes],
                send_sem=sum_send.at[g, k - 1],
                recv_sem=sum_recv.at[g, k - 1],
                device_id={f_axis: come},
                device_id_type=MESH,
            ).wait_recv()

    def origin(s, way):
        shift = -s if way == 0 else s
        return pick([order[(at[d] + shift) % n] for d in range(n)], me)

    def block_of(m, c, cn, block):
        return outs[m].at[pl.ds(c, cn), pl.ds(pl.multiple_of(block * rows, LANES), rows)]

    def ring_copies(g, s, way, sent):
        m, c0, cn = groups[g]
        block = origin(s if sent else s + 1, way)
        parts = [(c0, cn, False)]
        if s == half_ring - 1:
            half = middle(cn)
            parts = [(c0, half, False) if way == 0 else (c0 + half, cn - half, False)]
        elif g == last and s == half_ring - 2:
            parts = [(0, cut, way == 0), (cut, columns - cut, way == 1)]
            if way == 1:
                parts.reverse()
        copies = []
        for p, (c, k, kept) in enumerate(parts):
            place = block_of(m, c, k, block)
            copies.append(
                pltpu.make_async_remote_copy(
                    src_ref=nv.at[m, pl.ds(c, k)] if s == 0 and sent else place,
                    dst_ref=passed.at[pl.ds(c, k)] if kept else place,
                    send_sem=ring_send.at[g * half_ring + s + p, way],
                    recv_sem=ring_recv.at[g * half_ring + s + p, way],
                    device_id={f_axis: right if way == 0 else left},
                    device_id_type=MESH,
                )
            )
        return copies

    def ring_start(g, s):
        for pair in zip(ring_copies(g, s, 0, True), ring_copies(g, s, 1, True)):
            for copy in pair:
                copy.start()

    def norm_spread(k):
        return pltpu.make_async_remote_copy(
            src_ref=norm_buf.at[me, mw],
            dst_ref=norm_buf.at[me, mw],
            send_sem=nf_send.at[k - 1],
            recv_sem=nf_recv.at[k - 1],
            device_id={f_axis: lax.rem(me + k, n)},
            device_id_type=MESH,
        )

    def norm_pass(k, up, sent):
        held = mw - k if up else mw + k
        if not sent:
            held = held - 1 if up else held + 1
        place = norm_buf.at[:, held]
        return pltpu.make_async_remote_copy(
            src_ref=place,
            dst_ref=place,
            send_sem=nw_send.at[int(up)],
            recv_sem=nw_recv.at[k, int(up)],
            device_id={w_axis: mw + 1 if up else mw - 1},
            device_id_type=MESH,
        )

    def norm_gather():
        for k in range(1, n):
            come = lax.rem(me - k + n, n)
            pltpu.make_async_remote_copy(
                src_ref=norm_buf.at[come, mw],
                dst_ref=norm_buf.at[come, mw],
                send_sem=nf_send.at[k - 1],
                recv_sem=nf_recv.at[k - 1],
                device_id={f_axis: come},
                device_id_type=MESH,
            ).wait_recv()
        for k in range(w - 1):
            steps = (
                (True, jnp.logical_and(above, mw >= k), jnp.logical_and(below, mw >= k + 1)),
                (
                    False,
                    jnp.logical_and(below, mw + k < w),
                    jnp.logical_and(above, mw + k + 1 < w),
                ),
            )
            for up, sending, _ in steps:

                @pl.when(sending)
                def _():
                    norm_pass(k, up, True).start()

            for up, sending, coming in steps:

                @pl.when(coming)
                def _():
                    norm_pass(k, up, False).wait_recv()

                @pl.when(sending)
                def _():
                    norm_pass(k, up, True).wait_send()

        put(norm_buf, norm_out, small_sem.at[2])

    def put(source, place, sem):
        copy = pltpu.make_async_copy(source, place, sem)
        copy.start()
        puts.append(copy)

    def step(g):
        m, c0, cn = groups[g]
        for copy in loads[g]:
            copy.wait()
        if g < last:
            load(g + 1)
        blocks(c0, cn, functools.partial(step_block, m))
        if g == 0:
            pl.semaphore_wait(barrier, n - 1 + above.astype(jnp.int32) + below.astype(jnp.int32))
        exchange(g)
        if g == 0:
            for copy in norm_loads:
                copy.wait()
            norm_buf[me, mw] = norm_in[0, 0] + norm_in[1, 0]
            for k in range(1, n):
                copy = norm_spread(k)
                copy.start()
                sends.append(copy)

    def narrow(g):
        m, c0, cn = groups[g]
        exchanged(g)
        blocks(c0, cn, functools.partial(narrow_block, m))

    def keep(g):
        m, c0, cn = groups[g]
        put(tv.at[m, pl.ds(c0, cn)], wholes[m].at[pl.ds(c0, cn)], put_sem.at[g, 0])
        put(nv.at[m, pl.ds(c0, cn)], block_of(m, c0, cn, me), put_sem.at[g, 1])

    def receive(g, s):
        for way in (0, 1):
            for copy in ring_copies(g, s, way, False):
                copy.wait_recv()

    def forward(g, s):
        if s + 1 < half_ring and (g, s + 1) != (last, half_ring - 1):
            ring_start(g, s + 1)
        if (g, s) == (last, half_ring - 2):
            ranges = ((0, cut, right_piece), (cut, columns - cut, left_piece))
            for way, (c, k, piece) in enumerate(ranges):
                source = passed.at[pl.ds(c, k)]
                put(source, piece, piece_sem.at[way, 0])
                put(source, block_of(1, c, k, origin(s + 1, way)), piece_sem.at[way, 1])

    yields = lax.rem(mw, 2) == 0

    step(0)
    for g in range(len(groups)):
        if g < last:
            step(g + 1)
        narrow(g)
        if g < last:
            ring_start(g, 0)
        if g:
            keep(g - 1)

    @pl.when(jnp.logical_not(yields))
    def _():
        ring_start(last, 0)

    keep(last)
    put(scale_buf, scale_out, small_sem.at[3])

    norm_gather()
    for g in range(last):
        receive(g, 0)

    @pl.when(yields)
    def _():
        ring_start(last, 0)

    for g in range(last):
        forward(g, 0)
    for s in range(half_ring):
        for g in range(len(groups)):
            if (g, s) != (last, half_ring - 1) and (s > 0 or g == last):
                receive(g, s)
                forward(g, s)
    for copy in sends:
        copy.wait_send()
    for s in range(half_ring):
        for g in range(len(groups)):
            if (g, s) != (last, half_ring - 1):
                for way in (0, 1):
                    for copy in ring_copies(g, s, way, True):
                        copy.wait_send()
    for copy in puts:
        copy.wait()


def copy_kernel(*refs):
    half = len(refs) // 2
    for source, place in zip(refs[:half], refs[half:]):
        place[...] = source[...]


def place_kernel(n, order, f_axis, right_far, left_far, _, out, sem):
    cut, rows = right_far.shape
    me = lax.axis_index(f_axis)
    at = {d: i for i, d in enumerate(order)}
    far = pick([order[(at[d] + n // 2) % n] for d in range(n)], me)
    lanes = pl.ds(pl.multiple_of(far * rows, LANES), rows)
    ranges = ((right_far, 0, cut), (left_far, cut, left_far.shape[0]))
    copies = [
        pltpu.make_async_copy(piece, out.at[pl.ds(c, k), lanes], sem.at[i])
        for i, (piece, c, k) in enumerate(ranges)
    ]
    for copy in copies:
        copy.start()
    for copy in copies:
        copy.wait()


def solution(mesh):
    names = mesh.axis_names
    n, w = mesh.shape["fsdp"], mesh.shape["width"]
    order = ring_order(n)

    def shards(tg, dg, sg, tu, du, su, nt, ns):
        rows, columns = tg.shape
        padded = -(-columns // LANES) * LANES
        length = nt.shape[0]
        wide = -(-length // LANES) * LANES

        def line(x):
            return jnp.pad(x, (0, wide - length)).reshape(1, 1, wide)

        groups = len(groups_of(columns))
        hbm = pl.BlockSpec(memory_space=pl.ANY)
        vmem = pl.BlockSpec(memory_space=pltpu.VMEM)
        dma = pltpu.SemaphoreType.DMA
        sent = 3 * 2 * columns * rows * 2
        cut = middle(columns)
        bf16 = jnp.bfloat16
        out_g, out_u, whole_g, whole_u, right_piece, left_piece, scales, norm = pl.pallas_call(
            functools.partial(gather_kernel, n, w, order, names),
            out_shape=(
                jax.ShapeDtypeStruct((columns, n * rows), bf16),
                jax.ShapeDtypeStruct((columns, n * rows), bf16),
                jax.ShapeDtypeStruct((columns, rows), jnp.float32),
                jax.ShapeDtypeStruct((columns, rows), jnp.float32),
                jax.ShapeDtypeStruct((cut, rows), bf16),
                jax.ShapeDtypeStruct((columns - cut, rows), bf16),
                jax.ShapeDtypeStruct((2, 1, padded), jnp.float32),
                jax.ShapeDtypeStruct((n, w, 1, wide), jnp.float32),
            ),
            in_specs=[hbm] * 8,
            out_specs=[hbm] * 8,
            scratch_shapes=[
                pltpu.VMEM((2, columns, rows), jnp.float32),
                pltpu.VMEM((2, columns, rows), jnp.float32),
                pltpu.VMEM((2, columns, rows), jnp.float32),
                pltpu.VMEM((2, columns, rows), bf16),
                pltpu.VMEM((columns, rows), bf16),
                pltpu.VMEM((2, n, 1, padded), jnp.float32),
                pltpu.VMEM((LANES, LANES), jnp.float32),
                pltpu.VMEM((2, 1, padded), jnp.float32),
                pltpu.VMEM((2, 1, 1, wide), jnp.float32),
                pltpu.VMEM((n, w, 1, wide), jnp.float32),
                dma((3,)),
                dma((groups, 2)),
                dma((2, 2)),
                dma((4,)),
                dma((groups, n - 1)),
                dma((groups, n - 1)),
                dma((groups * (n // 2) + 1, 2)),
                dma((groups * (n // 2) + 1, 2)),
                dma((n - 1,)),
                dma((n - 1,)),
                dma((2,)),
                dma((w - 1, 2)),
            ],
            compiler_params=pltpu.CompilerParams(
                collective_id=0, has_side_effects=True, vmem_limit_bytes=60 * 1024 * 1024
            ),
            cost_estimate=pl.CostEstimate(
                flops=20 * columns * rows, bytes_accessed=16 * sent, transcendentals=0
            ),
        )(tg.T, dg.T, sg.T, tu.T, du.T, su.T, line(nt), line(ns))
        right_far, left_far = (
            lax.ppermute(piece, "fsdp", [(order[i], order[(i + sign) % n]) for i in range(n)])
            for piece, sign in ((right_piece, 1), (left_piece, -1))
        )
        moved = (out_g, out_u, whole_g, whole_u)
        specs = [pl.BlockSpec((LANES, x.shape[1]), lambda i: (i, 0)) for x in moved]
        out_g, out_u, whole_g, whole_u = pl.pallas_call(
            copy_kernel,
            grid=(-(-columns // LANES),),
            out_shape=tuple(jax.ShapeDtypeStruct(x.shape, x.dtype) for x in moved),
            in_specs=specs,
            out_specs=specs,
            compiler_params=pltpu.CompilerParams(vmem_limit_bytes=60 * 1024 * 1024),
            cost_estimate=pl.CostEstimate(
                flops=0, bytes_accessed=2 * sum(x.size * x.dtype.itemsize for x in moved), transcendentals=0
            ),
        )(*moved)
        out_u = pl.pallas_call(
            functools.partial(place_kernel, n, order, "fsdp"),
            out_shape=jax.ShapeDtypeStruct(out_u.shape, out_u.dtype),
            in_specs=[vmem, vmem, hbm],
            out_specs=hbm,
            input_output_aliases={2: 0},
            scratch_shapes=[dma((2,))],
            compiler_params=pltpu.CompilerParams(vmem_limit_bytes=16 * 1024 * 1024),
            cost_estimate=pl.CostEstimate(
                flops=0, bytes_accessed=4 * columns * rows, transcendentals=0
            ),
        )(right_far, left_far, out_u)
        serve_norm = norm[..., :length].reshape(n * w * length).astype(jnp.bfloat16)
        return (
            out_g.T,
            out_u.T,
            scales[0, 0, :columns],
            scales[1, 0, :columns],
            serve_norm,
            whole_g.T,
            whole_u.T,
        )

    split = P("fsdp", "width")
    flat = P(("fsdp", "width"))
    return jax.shard_map(
        shards,
        mesh=mesh,
        in_specs=(split,) * 6 + (flat,) * 2,
        out_specs=(P(None, "width"), P(None, "width"), P("width"), P("width"), P(), split, split),
        check_vma=False,
    )
```

profile of v0, /device:TPU:0, one launch (start us, length us, event | category | flops | bytes accessed | tf_op | source)
XLA Modules:
  0.0 194.3 jit_solution(1335502294768551851)
XLA Ops:
  0.6 160.6 %shard_map.135 = (bf16[1376,4096]{1,0:T(8,128)(2,1)}, bf16[1376,4096]{1,0:T(8,128)(2,1)}, f32[1376,1024]{1,0:T(8,128)}, f32[1376,1024]{1,0:T(8,128)}, bf16[688,1...) custom-call(f32[1376,1024]{1,0:T(8,128)} %bitcast.14, ...), custom_call_target="tpu_custom_call" | custom-call | flops 28180480 | bytes 270532608 | tf_op jit(solution)/shard_map/pallas_call | solution.py:412
  161.3 1.5 collective-permute-start
  162.8 0.6 collective-permute-start.1
  163.4 0.0 copy-start.1
  163.4 0.0 copy-start
  163.4 24.8 %shard_map.136 = (bf16[1376,4096]{1,0:T(8,128)(2,1)}, bf16[1376,4096]{1,0:T(8,128)(2,1)}, f32[1376,1024]{1,0:T(8,128)}, f32[1376,1024]{1,0:T(8,128)}) custom-call(bf16[1376,4096]{1,0:T(8,128)(2,1)} %get-tuple-element.19.refs_0_, bf16[1376,4096]{1,0:T(8,128)(2,1)} %get-tuple-element.20.refs_1_, f32[1376,1024]{1,0:T(8,128)} %get-tuple-element.21.refs_2_, ...), custom_call_target="tpu_custom_call" | custom-call | bytes 67633152 | tf_op jit(solution)/shard_map/pallas_call | solution.py:463
  188.2 0.0 copy-done.1
  188.2 0.6 slice_reduce_fusion
  188.8 0.0 copy-done
  188.8 0.6 convert_reduce_fusion
  189.5 1.8 collective-permute-done.right_far
  191.2 1.5 collective-permute-done.1.left_far
  192.7 1.6 shard_map.137
Async XLA Ops:
  161.3 30.0 %collective-permute-start = (bf16[688,1024]{1,0:T(8,128)(2,1)}, bf16[688,1024]{1,0:T(8,128)(2,1)S(1)}, u32[]{:S(2)}, u32[]{:S(2)}) collective-permute-start(bf16[688,1024]{1,0:T(8,128)(2,1)} %get-tuple-element.24), channel_id=1, source_target_pairs={{0,16},{16,24},{24,8},{8,0},{1,17},{17,25},{25,9},{9,1},{2,18},{18... | collective-permute-start | bytes 4227080 | tf_op jit(solution)/shard_map/ppermute | solution.py:458
  162.8 29.9 %collective-permute-start.1 = (bf16[688,1024]{1,0:T(8,128)(2,1)}, bf16[688,1024]{1,0:T(8,128)(2,1)S(1)}, u32[]{:S(2)}, u32[]{:S(2)}) collective-permute-start(bf16[688,1024]{1,0:T(8,128)(2,1)} %get-tuple-element.25), channel_id=1, source_target_pairs={{0,8},{16,0},{24,16},{8,24},{1,9},{17,1},{25,17},{9,25},{2,10},{18... | collective-permute-start | bytes 4227080 | tf_op jit(solution)/shard_map/ppermute | solution.py:458
  163.4 24.8 %copy-start.1 = (f32[2,1,1408]{2,1,0:T(1,128)S(1)}, f32[2,1,1408]{2,1,0:T(1,128)}, u32[]{:S(2)}) copy-start(f32[2,1,1408]{2,1,0:T(1,128)} %get-tuple-element.27) | copy-start | bytes 33796
  163.4 25.5 %copy-start = (f32[4,8,1,128]{3,2,1,0:T(1,128)S(1)}, f32[4,8,1,128]{3,2,1,0:T(1,128)}, u32[]{:S(2)}) copy-start(f32[4,8,1,128]{3,2,1,0:T(1,128)} %get-tuple-element.28) | copy-start | bytes 49156
where the time goes:
time: 194 us
  Pallas kernels  187 us (96%)
  waiting for transfers between devices  3.22 us (2%)
  starting transfers between devices  2.08 us (1%)
    pallas_call x1, Pallas kernels, shards(): pl.pallas_call(functools.partial(gather_kernel, n, w, order, names), out_...  161 us
    pallas_call x1, Pallas kernels, shards(): pl.pallas_call(copy_kernel, grid=(-(-columns // LANES),), out_shape=tuple...  24.8 us
  transfers between devices with their start and end apart: 2, of which 2 were waited for; matrix products, arithmetic and copies ran while one was open for 1% of the time, Pallas kernels for 13%

commit v1 on v0

--- a/solution.py
+++ b/solution.py
@@ -11,6 +11,8 @@
 hold_rate = 0.9
 LANES = 128
 SUB = 16
+CHUNK = 352
+RAW = 2 * SUB
 MESH = pl.DeviceIdType.MESH
 
 
@@ -40,20 +42,37 @@
     return gate + [(1, 0, columns)]
 
 
+def rings_of(columns):
+    (m, c0, cn), *others = groups_of(columns)
+    return [(m, c0, RAW), (m, c0 + RAW, cn - RAW), *others]
+
+
 def middle(columns):
     return columns // (2 * SUB) * SUB
 
 
+def tail_cut(columns):
+    return middle(columns) + SUB
+
+
+def pieces_of(columns):
+    cut = tail_cut(columns)
+    small = min(4 * SUB, cut // 2 // SUB * SUB)
+    return [(0, cut - small), (cut, columns - cut - small), (cut - small, small), (columns - small, small)]
+
+
 def gather_kernel(n, w, order, names, *refs):
     (tg, dg, sg, tu, du, su, nt, ns) = refs[:8]
-    (out_g, out_u, whole_g, whole_u, right_piece, left_piece, scale_out, norm_out) = refs[8:16]
-    (tv, dv, sv, nv, passed, sums, q, scale_buf, norm_in, norm_buf) = refs[16:26]
-    (in_sem, put_sem, piece_sem, small_sem, sum_send, sum_recv) = refs[26:32]
-    (ring_send, ring_recv, nf_send, nf_recv, nw_send, nw_recv) = refs[32:]
+    (out_g, out_u, whole_g, whole_u, scale_out, norm_out) = refs[8:14]
+    pieces, refs = refs[14:18], refs[18:]
+    (tv, dv, sv, nv, passed, sums, q, scale_buf, norm_in, norm_buf, raw_buf, near_buf) = refs[:12]
+    (in_sem, put_sem, piece_sem, small_sem, sum_send, sum_recv) = refs[12:18]
+    (ring_send, ring_recv, nf_send, nf_recv, nw_send, nw_recv) = refs[18:]
     f_axis, w_axis = names
     columns, rows = tg.shape
     groups = groups_of(columns)
-    last = len(groups) - 1
+    rings = rings_of(columns)
+    last, end = len(groups) - 1, len(rings) - 1
     args = ((tg, dg, sg), (tu, du, su))
     outs, wholes = (out_g, out_u), (whole_g, whole_u)
     me = lax.axis_index(f_axis)
@@ -62,7 +81,7 @@
     at = {d: i for i, d in enumerate(order)}
     right = pick([order[(at[d] + 1) % n] for d in range(n)], me)
     left = pick([order[(at[d] - 1) % n] for d in range(n)], me)
-    cut = middle(columns)
+    cut = tail_cut(columns)
 
     loads = {}
 
@@ -178,23 +197,29 @@
         return outs[m].at[pl.ds(c, cn), pl.ds(pl.multiple_of(block * rows, LANES), rows)]
 
     def ring_copies(g, s, way, sent):
-        m, c0, cn = groups[g]
+        m, c0, cn = rings[g]
         block = origin(s if sent else s + 1, way)
         parts = [(c0, cn, False)]
         if s == half_ring - 1:
             half = middle(cn)
             parts = [(c0, half, False) if way == 0 else (c0 + half, cn - half, False)]
-        elif g == last and s == half_ring - 2:
+        elif g == end and s == half_ring - 2:
             parts = [(0, cut, way == 0), (cut, columns - cut, way == 1)]
             if way == 1:
                 parts.reverse()
         copies = []
         for p, (c, k, kept) in enumerate(parts):
             place = block_of(m, c, k, block)
+            source = nv.at[m, pl.ds(c, k)] if s == 0 and sent else place
+            target = passed.at[pl.ds(c, k)] if kept else place
+            if g == 0 and s == 0:
+                source, target = tv.at[m, pl.ds(c, k)], raw_buf.at[way]
+            elif g == 0 and s == 1 and sent:
+                source = near_buf.at[way, pl.ds(c, k)]
             copies.append(
                 pltpu.make_async_remote_copy(
-                    src_ref=nv.at[m, pl.ds(c, k)] if s == 0 and sent else place,
-                    dst_ref=passed.at[pl.ds(c, k)] if kept else place,
+                    src_ref=source,
+                    dst_ref=target,
                     send_sem=ring_send.at[g * half_ring + s + p, way],
                     recv_sem=ring_recv.at[g * half_ring + s + p, way],
                     device_id={f_axis: right if way == 0 else left},
@@ -286,6 +311,7 @@
             pl.semaphore_wait(barrier, n - 1 + above.astype(jnp.int32) + below.astype(jnp.int32))
         exchange(g)
         if g == 0:
+            ring_start(0, 0)
             for copy in norm_loads:
                 copy.wait()
             norm_buf[me, mw] = norm_in[0, 0] + norm_in[1, 0]
@@ -304,20 +330,38 @@
         put(tv.at[m, pl.ds(c0, cn)], wholes[m].at[pl.ds(c0, cn)], put_sem.at[g, 0])
         put(nv.at[m, pl.ds(c0, cn)], block_of(m, c0, cn, me), put_sem.at[g, 1])
 
+    def sent(g, s):
+        for way in (0, 1):
+            for copy in ring_copies(g, s, way, True):
+                copy.wait_send()
+
     def receive(g, s):
         for way in (0, 1):
             for copy in ring_copies(g, s, way, False):
                 copy.wait_recv()
 
+    def narrow_near():
+        q[...] = jnp.broadcast_to(scale_buf[0, :, pl.ds(0, LANES)], (LANES, LANES)).T
+        for way in (0, 1):
+            for r in range(0, RAW, SUB):
+                at_rows = pl.ds(r, SUB)
+                by = q[at_rows, :]
+                for l in range(0, rows, LANES):
+                    lanes = pl.ds(l, LANES)
+                    near_buf[way, at_rows, lanes] = (raw_buf[way, at_rows, lanes] / by).astype(
+                        jnp.bfloat16
+                    )
+            put(near_buf.at[way], block_of(0, 0, RAW, origin(1, way)), small_sem.at[4 + way])
+
     def forward(g, s):
-        if s + 1 < half_ring and (g, s + 1) != (last, half_ring - 1):
+        if s + 1 < half_ring and (g, s + 1) != (end, half_ring - 1):
             ring_start(g, s + 1)
-        if (g, s) == (last, half_ring - 2):
-            ranges = ((0, cut, right_piece), (cut, columns - cut, left_piece))
-            for way, (c, k, piece) in enumerate(ranges):
-                source = passed.at[pl.ds(c, k)]
-                put(source, piece, piece_sem.at[way, 0])
-                put(source, block_of(1, c, k, origin(s + 1, way)), piece_sem.at[way, 1])
+        if (g, s) == (end, half_ring - 2):
+            for i, ((c, k), piece) in enumerate(zip(pieces_of(columns), pieces)):
+                put(passed.at[pl.ds(c, k)], piece, piece_sem.at[i])
+            for way, (c, k) in enumerate(((0, cut), (cut, columns - cut))):
+                near = block_of(1, c, k, origin(s + 1, way))
+                put(passed.at[pl.ds(c, k)], near, piece_sem.at[len(pieces) + way])
 
     yields = lax.rem(mw, 2) == 0
 
@@ -326,61 +370,100 @@
         if g < last:
             step(g + 1)
         narrow(g)
+        if g == last - 1:
+
+            @pl.when(yields)
+            def _():
+                sent(g, 0)
+
         if g < last:
-            ring_start(g, 0)
+            ring_start(g + 1, 0)
         if g:
             keep(g - 1)
 
     @pl.when(jnp.logical_not(yields))
     def _():
-        ring_start(last, 0)
+        ring_start(end, 0)
 
     keep(last)
     put(scale_buf, scale_out, small_sem.at[3])
 
     norm_gather()
-    for g in range(last):
+    for g in range(end):
         receive(g, 0)
+    narrow_near()
 
     @pl.when(yields)
     def _():
-        ring_start(last, 0)
-
-    for g in range(last):
+        ring_start(end, 0)
+
+    for g in range(end):
         forward(g, 0)
     for s in range(half_ring):
-        for g in range(len(groups)):
-            if (g, s) != (last, half_ring - 1) and (s > 0 or g == last):
+        for g in range(len(rings)):
+            if (g, s) != (end, half_ring - 1) and (s > 0 or g == end):
                 receive(g, s)
                 forward(g, s)
     for copy in sends:
         copy.wait_send()
     for s in range(half_ring):
-        for g in range(len(groups)):
-            if (g, s) != (last, half_ring - 1):
-                for way in (0, 1):
-                    for copy in ring_copies(g, s, way, True):
-                        copy.wait_send()
+        for g in range(len(rings)):
+            if (g, s) not in ((end, half_ring - 1), (last - 1, 0)):
+                sent(g, s)
+
+    @pl.when(jnp.logical_not(yields))
+    def _():
+        sent(last - 1, 0)
+
     for copy in puts:
         copy.wait()
 
 
-def copy_kernel(*refs):
-    half = len(refs) // 2
-    for source, place in zip(refs[:half], refs[half:]):
-        place[...] = source[...]
-
-
-def place_kernel(n, order, f_axis, right_far, left_far, _, out, sem):
-    cut, rows = right_far.shape
+def far_lanes(n, order, f_axis, rows, ahead):
     me = lax.axis_index(f_axis)
     at = {d: i for i, d in enumerate(order)}
-    far = pick([order[(at[d] + n // 2) % n] for d in range(n)], me)
-    lanes = pl.ds(pl.multiple_of(far * rows, LANES), rows)
-    ranges = ((right_far, 0, cut), (left_far, cut, left_far.shape[0]))
+    block = pick([order[(at[d] + n // 2 + ahead) % n] for d in range(n)], me)
+    return pl.ds(pl.multiple_of(block * rows, LANES), rows)
+
+
+def chunks_of(columns):
+    return [(c, min(CHUNK, columns - c)) for c in range(0, columns, CHUNK)]
+
+
+def copy_kernel(n, order, f_axis, *refs):
+    sources, places, held = refs[:4], refs[4:8], refs[8:11]
+    come_sem, go_sem = refs[11:]
+    columns, rows = sources[2].shape
+    moves = []
+    for c, k in chunks_of(columns):
+        at_rows = pl.ds(c, k)
+        moves += [(m + 2, (at_rows,), held[2].at[m, at_rows]) for m in range(2)]
+        moves.append((0, (at_rows,), held[0].at[at_rows]))
+        for b in range(1, n):
+            moves.append((1, (at_rows, far_lanes(n, order, f_axis, rows, b)), held[1].at[b - 1, at_rows]))
+    comes = [
+        pltpu.make_async_copy(sources[m].at[where], buf, come_sem.at[i])
+        for i, (m, where, buf) in enumerate(moves)
+    ]
+    goes = [
+        pltpu.make_async_copy(buf, places[m].at[where], go_sem.at[i])
+        for i, (m, where, buf) in enumerate(moves)
+    ]
+    for copy in comes:
+        copy.start()
+    for come, go in zip(comes, goes):
+        come.wait()
+        go.start()
+    for copy in goes:
+        copy.wait()
+
+
+def place_kernel(n, order, f_axis, starts, *refs):
+    pieces, out, sem = refs[: len(starts)], refs[-2], refs[-1]
+    lanes = far_lanes(n, order, f_axis, pieces[0].shape[1], 0)
     copies = [
-        pltpu.make_async_copy(piece, out.at[pl.ds(c, k), lanes], sem.at[i])
-        for i, (piece, c, k) in enumerate(ranges)
+        pltpu.make_async_copy(piece, out.at[pl.ds(c, piece.shape[0]), lanes], sem.at[i])
+        for i, (piece, c) in enumerate(zip(pieces, starts))
     ]
     for copy in copies:
         copy.start()
@@ -407,22 +490,21 @@
         vmem = pl.BlockSpec(memory_space=pltpu.VMEM)
         dma = pltpu.SemaphoreType.DMA
         sent = 3 * 2 * columns * rows * 2
-        cut = middle(columns)
+        pieces = pieces_of(columns)
         bf16 = jnp.bfloat16
-        out_g, out_u, whole_g, whole_u, right_piece, left_piece, scales, norm = pl.pallas_call(
+        out_g, out_u, whole_g, whole_u, scales, norm, *handed = pl.pallas_call(
             functools.partial(gather_kernel, n, w, order, names),
             out_shape=(
                 jax.ShapeDtypeStruct((columns, n * rows), bf16),
                 jax.ShapeDtypeStruct((columns, n * rows), bf16),
                 jax.ShapeDtypeStruct((columns, rows), jnp.float32),
                 jax.ShapeDtypeStruct((columns, rows), jnp.float32),
-                jax.ShapeDtypeStruct((cut, rows), bf16),
-                jax.ShapeDtypeStruct((columns - cut, rows), bf16),
                 jax.ShapeDtypeStruct((2, 1, padded), jnp.float32),
                 jax.ShapeDtypeStruct((n, w, 1, wide), jnp.float32),
+                *(jax.ShapeDtypeStruct((k, rows), bf16) for _, k in pieces),
             ),
             in_specs=[hbm] * 8,
-            out_specs=[hbm] * 8,
+            out_specs=[hbm] * (6 + len(pieces)),
             scratch_shapes=[
                 pltpu.VMEM((2, columns, rows), jnp.float32),
                 pltpu.VMEM((2, columns, rows), jnp.float32),
@@ -434,14 +516,16 @@
                 pltpu.VMEM((2, 1, padded), jnp.float32),
                 pltpu.VMEM((2, 1, 1, wide), jnp.float32),
                 pltpu.VMEM((n, w, 1, wide), jnp.float32),
+                pltpu.VMEM((2, RAW, rows), jnp.float32),
+                pltpu.VMEM((2, RAW, rows), bf16),
                 dma((3,)),
                 dma((groups, 2)),
-                dma((2, 2)),
-                dma((4,)),
+                dma((6,)),
+                dma((6,)),
                 dma((groups, n - 1)),
                 dma((groups, n - 1)),
-                dma((groups * (n // 2) + 1, 2)),
-                dma((groups * (n // 2) + 1, 2)),
+                dma(((groups + 1) * (n // 2) + 1, 2)),
+                dma(((groups + 1) * (n // 2) + 1, 2)),
                 dma((n - 1,)),
                 dma((n - 1,)),
                 dma((2,)),
@@ -454,35 +538,51 @@
                 flops=20 * columns * rows, bytes_accessed=16 * sent, transcendentals=0
             ),
         )(tg.T, dg.T, sg.T, tu.T, du.T, su.T, line(nt), line(ns))
-        right_far, left_far = (
-            lax.ppermute(piece, "fsdp", [(order[i], order[(i + sign) % n]) for i in range(n)])
-            for piece, sign in ((right_piece, 1), (left_piece, -1))
-        )
+
+        def travel(pair):
+            return [
+                lax.ppermute(piece, "fsdp", [(order[i], order[(i + sign) % n]) for i in range(n)])
+                for piece, sign in zip(pair, (1, -1))
+            ]
+
+        far = travel(handed[:2])
         moved = (out_g, out_u, whole_g, whole_u)
-        specs = [pl.BlockSpec((LANES, x.shape[1]), lambda i: (i, 0)) for x in moved]
+        count = len(chunks_of(columns)) * (n + 2)
         out_g, out_u, whole_g, whole_u = pl.pallas_call(
-            copy_kernel,
-            grid=(-(-columns // LANES),),
+            functools.partial(copy_kernel, n, order, "fsdp"),
             out_shape=tuple(jax.ShapeDtypeStruct(x.shape, x.dtype) for x in moved),
-            in_specs=specs,
-            out_specs=specs,
+            in_specs=[hbm] * 4,
+            out_specs=[hbm] * 4,
+            scratch_shapes=[
+                pltpu.VMEM((columns, n * rows), bf16),
+                pltpu.VMEM((n - 1, columns, rows), bf16),
+                pltpu.VMEM((2, columns, rows), jnp.float32),
+                dma((count,)),
+                dma((count,)),
+            ],
             compiler_params=pltpu.CompilerParams(vmem_limit_bytes=60 * 1024 * 1024),
             cost_estimate=pl.CostEstimate(
                 flops=0, bytes_accessed=2 * sum(x.size * x.dtype.itemsize for x in moved), transcendentals=0
             ),
         )(*moved)
-        out_u = pl.pallas_call(
-            functools.partial(place_kernel, n, order, "fsdp"),
-            out_shape=jax.ShapeDtypeStruct(out_u.shape, out_u.dtype),
-            in_specs=[vmem, vmem, hbm],
-            out_specs=hbm,
-            input_output_aliases={2: 0},
-            scratch_shapes=[dma((2,))],
-            compiler_params=pltpu.CompilerParams(vmem_limit_bytes=16 * 1024 * 1024),
-            cost_estimate=pl.CostEstimate(
-                flops=0, bytes_accessed=4 * columns * rows, transcendentals=0
-            ),
-        )(right_far, left_far, out_u)
+        out_u, *rest = lax.optimization_barrier((out_u, *handed[2:]))
+        far += travel(rest)
+        for first in range(0, len(far), 2):
+            landed = far[first : first + 2]
+            out_u = pl.pallas_call(
+                functools.partial(
+                    place_kernel, n, order, "fsdp", [c for c, _ in pieces[first : first + 2]]
+                ),
+                out_shape=jax.ShapeDtypeStruct(out_u.shape, out_u.dtype),
+                in_specs=[vmem, vmem, hbm],
+                out_specs=hbm,
+                input_output_aliases={2: 0},
+                scratch_shapes=[dma((2,))],
+                compiler_params=pltpu.CompilerParams(vmem_limit_bytes=16 * 1024 * 1024),
+                cost_estimate=pl.CostEstimate(
+                    flops=0, bytes_accessed=2 * sum(2 * x.size for x in landed), transcendentals=0
+                ),
+            )(*landed, out_u)
         serve_norm = norm[..., :length].reshape(n * w * length).astype(jnp.bfloat16)
         return (
             out_g.T,

time: 194 us -> 191 us (0.985)
  Pallas kernels: 187 us -> 184 us
  starting transfers between devices: 2.08 us -> 4.16 us
    pallas_call x2 -> x3, Pallas kernels: 26.4 us -> 23.4 us  [the longest x1 21.2 us: shards(): pl.pallas_call(functools.partial(copy_kernel, n, order, 'fsdp'), out_shap...]
    ppermute x2 -> x4, starting transfers between devices: 2.08 us -> 4.16 us  [travel(): lax.ppermute(piece, 'fsdp', [(order[i], order[(i + sign) % n]) for i in r...]
  transfers between devices with their start and end apart: 2 -> 4, of which waited for: 2 -> 1; matrix products, arithmetic and copies ran while one was open for 1% -> 1% of each run, Pallas kernels for 13% -> 12%
where the time goes in v1:
time: 191 us
  Pallas kernels  184 us (96%)
  starting transfers between devices  4.16 us (2%)
    pallas_call x1, Pallas kernels, shards(): pl.pallas_call(functools.partial(gather_kernel, n, w, order, names), out_...  160 us
    pallas_call x1, Pallas kernels, shards(): pl.pallas_call(functools.partial(copy_kernel, n, order, 'fsdp'), out_shap...  21.2 us
    ppermute x4, starting transfers between devices, travel(): lax.ppermute(piece, 'fsdp', [(order[i], order[(i + sign) % n]) for i in r...  4.16 us
  transfers between devices with their start and end apart: 4, of which 1 were waited for; matrix products, arithmetic and copies ran while one was open for 1% of the time, Pallas kernels for 12%

profile of v1, /device:TPU:0, one launch (start us, length us, event | category | flops | bytes accessed | tf_op | source)
XLA Modules:
  0.0 191.3 jit_solution(14771108619283313960)
XLA Ops:
  0.6 160.1 %shard_map.135 = (bf16[1376,4096]{1,0:T(8,128)(2,1)}, bf16[1376,4096]{1,0:T(8,128)(2,1)}, f32[1376,1024]{1,0:T(8,128)}, f32[1376,1024]{1,0:T(8,128)}, f32[2,1,14...) custom-call(f32[1376,1024]{1,0:T(8,128)} %bitcast.14, ...), custom_call_target="tpu_custom_call" | custom-call | flops 28180480 | bytes 270532608 | tf_op jit(solution)/shard_map/pallas_call | solution.py:495
  160.8 1.5 collective-permute-start.2
  162.3 0.6 collective-permute-start.3
  162.8 0.0 copy-start.3
  162.8 0.0 copy-start.2
  162.8 0.0 copy-start.1
  162.8 0.0 copy-start
  162.8 21.2 %shard_map.136 = (bf16[1376,4096]{1,0:T(8,128)(2,1)}, bf16[1376,4096]{1,0:T(8,128)(2,1)}, f32[1376,1024]{1,0:T(8,128)}, f32[1376,1024]{1,0:T(8,128)}) custom-call(bf16[1376,4096]{1,0:T(8,128)(2,1)} %get-tuple-element.24.refs_0_, bf16[1376,4096]{1,0:T(8,128)(2,1)} %get-tuple-element.25.refs_1_, f32[1376,1024]{1,0:T(8,128)} %get-tuple-element.26.refs_2_, ...), custom_call_target="tpu_custom_call" | custom-call | bytes 67633152 | tf_op jit(solution)/shard_map/pallas_call | solution.py:551
  184.1 0.0 copy-done.3
  184.1 1.5 collective-permute-start
  185.6 0.0 copy-done.2
  185.6 0.6 collective-permute-start.1
  186.2 0.0 copy-done.1
  186.2 0.6 slice_reduce_fusion
  186.8 0.0 copy-done
  186.8 0.6 convert_reduce_fusion
  187.4 1.6 collective-permute-done.3.refs_1_
  189.0 0.0 collective-permute-done.2.refs_0_
  189.0 1.5 shard_map.137.refs_2_
  190.5 0.0 collective-permute-done.refs_0_
  190.5 0.0 collective-permute-done.1.refs_1_
  190.5 0.7 shard_map.138
Async XLA Ops:
  160.8 28.3 %collective-permute-start.2 = (bf16[640,1024]{1,0:T(8,128)(2,1)}, bf16[640,1024]{1,0:T(8,128)(2,1)S(1)}, u32[]{:S(2)}, u32[]{:S(2)}) collective-permute-start(bf16[640,1024]{1,0:T(8,128)(2,1)} %get-tuple-element.34), channel_id=1, source_target_pairs={{0,16},{16,24},{24,8},{8,0},{1,17},{17,25},{25,9},{9,1},{2,18},{18... | collective-permute-start | bytes 3932168 | tf_op jit(solution)/shard_map/ppermute | solution.py:544
  162.3 26.8 %collective-permute-start.3 = (bf16[608,1024]{1,0:T(8,128)(2,1)}, bf16[608,1024]{1,0:T(8,128)(2,1)S(1)}, u32[]{:S(2)}, u32[]{:S(2)}) collective-permute-start(bf16[608,1024]{1,0:T(8,128)(2,1)} %get-tuple-element.35), channel_id=1, source_target_pairs={{0,8},{16,0},{24,16},{8,24},{1,9},{17,1},{25,17},{9,25},{2,10},{18... | collective-permute-start | bytes 3735560 | tf_op jit(solution)/shard_map/ppermute | solution.py:544
  162.8 21.2 %copy-start.3 = (bf16[64,1024]{1,0:T(8,128)(2,1)S(1)}, bf16[64,1024]{1,0:T(8,128)(2,1)}, u32[]{:S(2)}) copy-start(bf16[64,1024]{1,0:T(8,128)(2,1)} %get-tuple-element.32) | copy-start | bytes 393220
  162.8 22.7 %copy-start.2 = (bf16[64,1024]{1,0:T(8,128)(2,1)S(1)}, bf16[64,1024]{1,0:T(8,128)(2,1)}, u32[]{:S(2)}) copy-start(bf16[64,1024]{1,0:T(8,128)(2,1)} %get-tuple-element.33) | copy-start | bytes 393220
  162.8 23.3 %copy-start.1 = (f32[2,1,1408]{2,1,0:T(1,128)S(1)}, f32[2,1,1408]{2,1,0:T(1,128)}, u32[]{:S(2)}) copy-start(f32[2,1,1408]{2,1,0:T(1,128)} %get-tuple-element.37) | copy-start | bytes 33796
  162.8 23.9 %copy-start = (f32[4,8,1,128]{3,2,1,0:T(1,128)S(1)}, f32[4,8,1,128]{3,2,1,0:T(1,128)}, u32[]{:S(2)}) copy-start(f32[4,8,1,128]{3,2,1,0:T(1,128)} %get-tuple-element.38) | copy-start | bytes 49156
  184.1 6.5 %collective-permute-start = (bf16[64,1024]{1,0:T(8,128)(2,1)S(1)}, bf16[64,1024]{1,0:T(8,128)(2,1)S(1)}, u32[]{:S(2)}, u32[]{:S(2)}) collective-permute-start(bf16[64,1024]{1,0:T(8,128)(2,1)S(1)} %copy-done.3), channel_id=1, source_target_pairs={{0,16},{16,24},{24,8},{8,0},{1,17},{17,25},{25,9},{9,1},{2,18},{18... | collective-permute-start | bytes 393224 | tf_op jit(solution)/shard_map/ppermute | solution.py:544
  185.6 5.0 %collective-permute-start.1 = (bf16[64,1024]{1,0:T(8,128)(2,1)S(1)}, bf16[64,1024]{1,0:T(8,128)(2,1)S(1)}, u32[]{:S(2)}, u32[]{:S(2)}) collective-permute-start(bf16[64,1024]{1,0:T(8,128)(2,1)S(1)} %copy-done.2), channel_id=1, source_target_pairs={{0,8},{16,0},{24,16},{8,24},{1,9},{17,1},{25,17},{9,25},{2,10},{18... | collective-permute-start | bytes 393224 | tf_op jit(solution)/shard_map/ppermute | solution.py:544

commit v2 on v1

--- a/solution.py
+++ b/solution.py
@@ -52,7 +52,7 @@
 
 
 def tail_cut(columns):
-    return middle(columns) + SUB
+    return middle(columns)
 
 
 def pieces_of(columns):
@@ -330,11 +330,6 @@
         put(tv.at[m, pl.ds(c0, cn)], wholes[m].at[pl.ds(c0, cn)], put_sem.at[g, 0])
         put(nv.at[m, pl.ds(c0, cn)], block_of(m, c0, cn, me), put_sem.at[g, 1])
 
-    def sent(g, s):
-        for way in (0, 1):
-            for copy in ring_copies(g, s, way, True):
-                copy.wait_send()
-
     def receive(g, s):
         for way in (0, 1):
             for copy in ring_copies(g, s, way, False):
@@ -363,18 +358,19 @@
                 near = block_of(1, c, k, origin(s + 1, way))
                 put(passed.at[pl.ds(c, k)], near, piece_sem.at[len(pieces) + way])
 
-    yields = lax.rem(mw, 2) == 0
+    yields = lax.rem(mw, 2) == 1
 
     step(0)
     for g in range(len(groups)):
         if g < last:
             step(g + 1)
         narrow(g)
-        if g == last - 1:
+        if 0 < g < last:
 
             @pl.when(yields)
             def _():
-                sent(g, 0)
+                for before in (0, 1) if g == 1 else (g,):
+                    receive(before, 0)
 
         if g < last:
             ring_start(g + 1, 0)
@@ -389,32 +385,45 @@
     put(scale_buf, scale_out, small_sem.at[3])
 
     norm_gather()
-    for g in range(end):
-        receive(g, 0)
+
+    @pl.when(jnp.logical_not(yields))
+    def _():
+        for before in range(last):
+            receive(before, 0)
+
+    receive(last, 0)
     narrow_near()
 
     @pl.when(yields)
     def _():
         ring_start(end, 0)
 
-    for g in range(end):
-        forward(g, 0)
-    for s in range(half_ring):
+    @pl.when(jnp.logical_not(yields))
+    def _():
+        for g in range(end):
+            forward(g, 0)
+
+    receive(end, 0)
+
+    @pl.when(yields)
+    def _():
+        for g in range(end):
+            forward(g, 0)
+
+    forward(end, 0)
+    for s in range(1, half_ring):
         for g in range(len(rings)):
-            if (g, s) != (end, half_ring - 1) and (s > 0 or g == end):
+            if (g, s) != (end, half_ring - 1):
                 receive(g, s)
                 forward(g, s)
     for copy in sends:
         copy.wait_send()
     for s in range(half_ring):
         for g in range(len(rings)):
-            if (g, s) not in ((end, half_ring - 1), (last - 1, 0)):
-                sent(g, s)
-
-    @pl.when(jnp.logical_not(yields))
-    def _():
-        sent(last - 1, 0)
-
+            if (g, s) != (end, half_ring - 1):
+                for way in (0, 1):
+                    for copy in ring_copies(g, s, way, True):
+                        copy.wait_send()
     for copy in puts:
         copy.wait()
 

time: 191 us -> 191 us (level)
  the two profiles are of different devices: /device:TPU:0 before, /device:TPU:1 now
where the time goes in v2:
time: 191 us
  Pallas kernels  185 us (97%)
  starting transfers between devices  3.19 us (2%)
    pallas_call x1, Pallas kernels, shards(): pl.pallas_call(functools.partial(gather_kernel, n, w, order, names), out_...  161 us
    pallas_call x1, Pallas kernels, shards(): pl.pallas_call(functools.partial(copy_kernel, n, order, 'fsdp'), out_shap...  21.2 us
  transfers between devices with their start and end apart: 4, of which 2 were waited for; matrix products, arithmetic and copies ran while one was open for 1% of the time, Pallas kernels for 12%

profile of v2, /device:TPU:1, one launch (start us, length us, event | category | flops | bytes accessed | tf_op | source)
XLA Modules:
  0.0 190.7 jit_solution(4064277325387716708)
XLA Ops:
  0.6 161.3 %shard_map.135 = (bf16[1376,4096]{1,0:T(8,128)(2,1)}, bf16[1376,4096]{1,0:T(8,128)(2,1)}, f32[1376,1024]{1,0:T(8,128)}, f32[1376,1024]{1,0:T(8,128)}, f32[2,1,14...) custom-call(f32[1376,1024]{1,0:T(8,128)} %bitcast.14, ...), custom_call_target="tpu_custom_call" | custom-call | flops 28180480 | bytes 270532608 | tf_op jit(solution)/shard_map/pallas_call | solution.py:504
  161.9 0.1 collective-permute-start.2
  162.0 1.6 collective-permute-start.3
  163.6 0.0 copy-start.3
  163.6 0.0 copy-start.2
  163.6 0.0 copy-start.1
  163.6 0.0 copy-start
  163.6 21.2 %shard_map.136 = (bf16[1376,4096]{1,0:T(8,128)(2,1)}, bf16[1376,4096]{1,0:T(8,128)(2,1)}, f32[1376,1024]{1,0:T(8,128)}, f32[1376,1024]{1,0:T(8,128)}) custom-call(bf16[1376,4096]{1,0:T(8,128)(2,1)} %get-tuple-element.24.refs_0_, bf16[1376,4096]{1,0:T(8,128)(2,1)} %get-tuple-element.25.refs_1_, f32[1376,1024]{1,0:T(8,128)} %get-tuple-element.26.refs_2_, ...), custom_call_target="tpu_custom_call" | custom-call | bytes 67633152 | tf_op jit(solution)/shard_map/pallas_call | solution.py:560
  184.8 0.0 copy-done.3
  184.8 0.1 collective-permute-start
  184.9 0.0 copy-done.2
  184.9 1.5 collective-permute-start.1
  186.3 0.0 copy-done.1
  186.3 0.6 slice_reduce_fusion
  187.0 0.0 copy-done
  187.0 0.6 convert_reduce_fusion
  187.6 0.8 collective-permute-done.2.refs_0_
  188.4 0.1 collective-permute-done.3.refs_1_
  188.5 1.5 shard_map.137.refs_2_
  189.9 0.0 collective-permute-done.refs_0_
  190.0 0.0 collective-permute-done.1.refs_1_
  190.0 0.7 shard_map.138
Async XLA Ops:
  161.9 26.5 %collective-permute-start.2 = (bf16[624,1024]{1,0:T(8,128)(2,1)}, bf16[624,1024]{1,0:T(8,128)(2,1)S(1)}, u32[]{:S(2)}, u32[]{:S(2)}) collective-permute-start(bf16[624,1024]{1,0:T(8,128)(2,1)} %get-tuple-element.34), channel_id=1, source_target_pairs={{0,16},{16,24},{24,8},{8,0},{1,17},{17,25},{25,9},{9,1},{2,18},{18... | collective-permute-start | bytes 3833864 | tf_op jit(solution)/shard_map/ppermute | solution.py:553
  162.0 26.5 %collective-permute-start.3 = (bf16[624,1024]{1,0:T(8,128)(2,1)}, bf16[624,1024]{1,0:T(8,128)(2,1)S(1)}, u32[]{:S(2)}, u32[]{:S(2)}) collective-permute-start(bf16[624,1024]{1,0:T(8,128)(2,1)} %get-tuple-element.35), channel_id=1, source_target_pairs={{0,8},{16,0},{24,16},{8,24},{1,9},{17,1},{25,17},{9,25},{2,10},{18... | collective-permute-start | bytes 3833864 | tf_op jit(solution)/shard_map/ppermute | solution.py:553
  163.6 21.2 %copy-start.3 = (bf16[64,1024]{1,0:T(8,128)(2,1)S(1)}, bf16[64,1024]{1,0:T(8,128)(2,1)}, u32[]{:S(2)}) copy-start(bf16[64,1024]{1,0:T(8,128)(2,1)} %get-tuple-element.32) | copy-start | bytes 393220
  163.6 21.3 %copy-start.2 = (bf16[64,1024]{1,0:T(8,128)(2,1)S(1)}, bf16[64,1024]{1,0:T(8,128)(2,1)}, u32[]{:S(2)}) copy-start(bf16[64,1024]{1,0:T(8,128)(2,1)} %get-tuple-element.33) | copy-start | bytes 393220
  163.6 22.8 %copy-start.1 = (f32[2,1,1408]{2,1,0:T(1,128)S(1)}, f32[2,1,1408]{2,1,0:T(1,128)}, u32[]{:S(2)}) copy-start(f32[2,1,1408]{2,1,0:T(1,128)} %get-tuple-element.37) | copy-start | bytes 33796
  163.6 23.4 %copy-start = (f32[4,8,1,128]{3,2,1,0:T(1,128)S(1)}, f32[4,8,1,128]{3,2,1,0:T(1,128)}, u32[]{:S(2)}) copy-start(f32[4,8,1,128]{3,2,1,0:T(1,128)} %get-tuple-element.38) | copy-start | bytes 49156
  184.8 5.1 %collective-permute-start = (bf16[64,1024]{1,0:T(8,128)(2,1)S(1)}, bf16[64,1024]{1,0:T(8,128)(2,1)S(1)}, u32[]{:S(2)}, u32[]{:S(2)}) collective-permute-start(bf16[64,1024]{1,0:T(8,128)(2,1)S(1)} %copy-done.3), channel_id=1, source_target_pairs={{0,16},{16,24},{24,8},{8,0},{1,17},{17,25},{25,9},{9,1},{2,18},{18... | collective-permute-start | bytes 393224 | tf_op jit(solution)/shard_map/ppermute | solution.py:553
  184.9 5.1 %collective-permute-start.1 = (bf16[64,1024]{1,0:T(8,128)(2,1)S(1)}, bf16[64,1024]{1,0:T(8,128)(2,1)S(1)}, u32[]{:S(2)}, u32[]{:S(2)}) collective-permute-start(bf16[64,1024]{1,0:T(8,128)(2,1)S(1)} %copy-done.2), channel_id=1, source_target_pairs={{0,8},{16,0},{24,16},{8,24},{1,9},{17,1},{25,17},{9,25},{2,10},{18... | collective-permute-start | bytes 393224 | tf_op jit(solution)/shard_map/ppermute | solution.py:553
